TPU v7x, 32 devices: a whole 2x2x4 slice. The times are simulated.
32 devices in a mesh: head: 8 (over y, x, core), seq: 4 (over z).
Axes of the slice: x: 2, y: 2, z: 4, core: 2. Of those that a mesh axis runs over, the one named last changes fastest.
Arguments:
- query_rows: bfloat16 [512, 16384], P('seq', 'head'), may hold values from -512 to 512
- key_rows: bfloat16 [512, 1024], P('seq'), may hold values from -32 to 32
- value_rows: bfloat16 [512, 1024], P('seq'), may hold values from -6 to 6
- positions: int32 [512], P('seq'), may hold values from 0 to 511, as said below
Outputs:
- attended: bfloat16 [512, 16384], P('seq', 'head')
- hessian: float32 [16384, 16384], P('head', 'seq')
Inputs may be any that keep to these rules, and one draw needn't show every extreme that they name: Each aligned block of 4 spans of 128 tokens is one sequence; each span holds 128 consecutive ascending positions starting at a multiple of 128, and the sequence's spans together hold every position 0 to 511 once.
All inputs are finite; a program needn't handle non-finite values.
Results may differ from a plain program's by a relative error of at most 0.0037.
Values may be sent and summed in bfloat16 or wider, within the bound.
A program may use at most 128 MiB of HBM per device.

v0:
```python
import jax
import jax.numpy as jnp
from jax import lax
from jax.sharding import PartitionSpec as P

HEADS = 128
KVH = 8
HD = 128
SPANS = 4


def from_partner(value, axis, stride):
    mask = 2**stride
    pairs = [(source, source ^ mask) for source in range(lax.axis_size(axis))]
    return lax.ppermute(value, axis, pairs)


def spread(x, axis, root):
    mine = lax.axis_index(axis) == root
    return lax.psum(jnp.where(mine, x, jnp.zeros_like(x)), axis)


def attend_block(queries, key_block, value_block, visible, local_heads, local_tokens, score_scale):
    scores = jnp.dot(queries, key_block.T, preferred_element_type=jnp.float32) * score_scale
    scores = scores.reshape(local_heads, local_tokens, key_block.shape[0])
    masked = jnp.where(visible[None], scores, -jnp.inf)
    row_top = jnp.max(masked, axis=2, keepdims=True)
    weights = jnp.exp(masked - row_top)
    weight_sum = jnp.sum(weights, axis=2, keepdims=True)
    mixed = jnp.dot(
        weights.astype(jnp.bfloat16).reshape(local_heads * local_tokens, key_block.shape[0]),
        value_block,
        preferred_element_type=jnp.float32,
    )
    return mixed.reshape(local_heads, local_tokens, HD) / weight_sum


def on_device(query_rows, key_rows, value_rows, positions):
    local_tokens = query_rows.shape[0]
    local_heads = query_rows.shape[1] // HD
    group_size = HEADS // KVH
    score_scale = HD ** (-0.5)
    head_index = lax.axis_index("head")
    span_index = lax.axis_index("seq")
    seq_devices = lax.axis_size("seq")
    head_devices = lax.axis_size("head")
    key_head = head_index * local_heads // group_size
    key_slice = lax.dynamic_slice_in_dim(key_rows, key_head * HD, HD, 1)
    value_slice = lax.dynamic_slice_in_dim(value_rows, key_head * HD, HD, 1)
    queries = jnp.transpose(query_rows.reshape(local_tokens, local_heads, HD), (1, 0, 2))
    queries = queries.reshape(local_heads * local_tokens, HD)
    key_block, value_block, place_block = (key_slice, value_slice, positions)
    for bit in range(SPANS.bit_length() - 1):
        other_keys, other_values, other_places = from_partner(
            (key_block, value_block, place_block), "seq", bit
        )
        key_block = jnp.concatenate([key_block, other_keys], axis=0)
        value_block = jnp.concatenate([value_block, other_values], axis=0)
        place_block = jnp.concatenate([place_block, other_places], axis=0)
    visible = place_block[None, :] <= positions[:, None]
    outcome = attend_block(
        queries, key_block, value_block, visible, local_heads, local_tokens, score_scale
    )
    attended = (
        jnp.transpose(outcome, (1, 0, 2))
        .reshape(local_tokens, local_heads * HD)
        .astype(jnp.bfloat16)
    )
    row_operand = lax.all_gather(attended, "seq", axis=0, tiled=True)
    root_count = head_devices // seq_devices
    column_parts = []
    for offset in range(root_count):
        column_parts.append(spread(row_operand, "head", span_index * root_count + offset))
    columns = jnp.concatenate(column_parts, axis=1)
    hessian = lax.dot_general(
        row_operand, columns, (((0,), (0,)), ((), ())), preferred_element_type=jnp.float32
    )
    return (attended, hessian)


def solution(mesh):
    placed = (P("seq", "head"), P("seq", None), P("seq", None), P("seq"))
    return jax.shard_map(
        on_device,
        mesh=mesh,
        in_specs=placed,
        out_specs=(P("seq", "head"), P("head", "seq")),
        check_vma=False,
    )
```

profile of v0, /device:TPU:0, one launch (start us, length us, event | category | flops | bytes accessed | tf_op | source)
XLA Modules:
  0.0 186.5 jit_solution(7501032044831482604)
XLA Ops:
  7.2 0.0 copy-start
  7.2 0.0 copy-start.3
  7.2 0.0 all-gather.2.cloned.1.call-start
  7.2 3.1 %collective-permute-start = (s32[128]{0:T(128)}, s32[128]{0:T(128)S(1)}, u32[]{:S(2)}, u32[]{:S(2)}) collective-permute-start(s32[128]{0:T(128)} %param.7), channel_id=1, source_target_pairs={{0,1},{1,0},{2,3},{3,2},{4,5},{5,4},{6,7},{7,6},{8,9},{9,8},{10,11... | collective-permute-start | bytes 1544 | tf_op jit(solution)/shard_map/ppermute | solution.py:15
  10.4 0.0 copy-done
  10.4 0.1 copy.18
  10.5 0.9 collective-permute-start.4
  11.4 0.7 collective-permute-done
  12.0 0.7 pad_add_fusion.1
  12.7 3.0 %collective-permute-start.1 = (s32[256]{0:T(256)S(1)}, s32[256]{0:T(256)S(1)}, u32[]{:S(2)}, u32[]{:S(2)}) collective-permute-start(s32[256]{0:T(256)S(1)} %pad_add_fusion.1), channel_id=1, source_target_pairs={{0,2},{1,3},{2,0},{3,1},{4,6},{5,7},{6,4},{7,5},{8,10},{9,11},{10,... | collective-permute-start | bytes 3080 | tf_op jit(solution)/shard_map/ppermute | solution.py:15
  15.7 0.8 constant_dynamic-slice_fusion.1
  16.5 1.6 collective-permute-start.2
  18.1 1.3 copy.12
  19.4 0.3 copy.13
  19.7 0.0 collective-permute-done.1
  19.7 0.0 copy-done.3
  19.7 0.1 broadcast_compare_fusion
  19.9 0.6 collective-permute-done.2
  20.4 0.1 collective-permute-start.3
  20.5 0.0 collective-permute-done.4
  20.5 2.9 %collective-permute-start.5 = (bf16[256,128]{0,1:T(8,128)(2,1)S(1)}, bf16[256,128]{0,1:T(8,128)(2,1)S(1)}, u32[]{:S(2)}, u32[]{:S(2)}) collective-permute-start(bf16[256,128]{0,1:T(8,128)(2,1)S(1)} %pad_maximum_fusion.1), channel_id=1, source_target_pairs={{0,2},{1,3},{2,0},{3,1},{4,6},{5,7},{6,4},{7,5},{8,10},{9,11},{10,... | collective-permute-start | bytes 196616 | tf_op jit(solution)/shard_map/ppermute | solution.py:15
  23.4 2.2 %collective-permute-done.3 = bf16[256,128]{1,0:T(8,128)(2,1)S(1)} collective-permute-done((bf16[256,128]{1,0:T(8,128)(2,1)S(1)}, bf16[256,128]{1,0:T(8,128)(2,1)S(1)}, u32[]{:S(2)}, u32[]{:S(2)}) %collective-permute-start.3) | collective-permute-done | bytes 65568 | tf_op jit(solution)/shard_map/ppermute | solution.py:15
  25.6 0.3 broadcast_in_dim.19
  25.9 1.0 fusion.20
  26.8 0.7 fusion.4
  27.5 2.5 %copy.17 = bf16[2048,512]{1,0:T(8,128)(2,1)} copy(bf16[2048,512]{0,1:T(8,128)(2,1)S(1)} %get-tuple-element.11) | data formatting | bytes 4194304 | tf_op jit(solution)/shard_map/dot_general | solution.py:30
  30.0 0.0 collective-permute-done.5
  30.0 3.2 %fusion.7 = bf16[128,16,128]{0,2,1:T(8,128)(2,1)} fusion(bf16[16,128,512]{2,1,0:T(8,128)(2,1)} %bitcast.28, f32[128,16]{0,1:T(8,128)S(1)} %bitcast.34, bf16[256,128]{0,1:T(8,128)(2,1)S(1)} %collective-permute-done.5, bf16[128,128]{0,1:T(8,128)(2,1)S(1)} %collective-permute-done.4, bf16[128,128]{0,1:T(8,128)(2,1)S(1)} %copy.18), kind=kOutput, calls=%fused_computation.12 | convolution fusion | flops 269352960 | bytes 2760704 | tf_op jit(solution)/shard_map/dot_general | solution.py:30
  33.2 0.0 all-gather.2.cloned.1.call-update
  33.2 0.0 all-reduce.3.cloned.1.call-start
  33.3 46.2 %all-gather.2.cloned.1.call-done = bf16[512,2048]{0,1:T(8,128)(2,1)} async-done(((bf16[128,2048]{0,1:T(8,128)(2,1)}), bf16[512,2048]{0,1:T(8,128)(2,1)}) %all-gather.2.cloned.1.call-update) | async-done | bytes 2097168 | tf_op jit(solution)/shard_map/all_gather | solution.py:69
  79.5 3.9 %broadcast_select_fusion.1 = (bf16[512,2048]{0,1:T(8,128)(2,1)}, bf16[512,2048]{0,1:T(8,128)(2,1)}) fusion(bf16[512,2048]{0,1:T(8,128)(2,1)} %all-gather.2.cloned.1.call-done, pred[]{:T(512)S(6)} %eq.6, pred[]{:T(512)S(6)} %eq.7), kind=kLoop, calls=%fused_computation.9 | loop fusion | flops 2097152 | bytes 6291458 | tf_op jit(solution)/shard_map/jit(_where)/select_n | solution.py:20
  83.4 0.0 copy-start.2
  83.4 0.0 copy-start.1
  83.4 0.0 all-reduce.3.cloned.1.call-update
  83.4 1.0 copy-done.2
  84.4 1.0 copy.16
  85.4 77.2 %all-reduce.3.cloned.1.call-done = (bf16[512,2048]{0,1:T(8,128)(2,1)}, bf16[512,2048]{0,1:T(8,128)(2,1)}) async-done(((bf16[512,2048]{0,1:T(8,128)(2,1)}, bf16[512,2048]{0,1:T(8,128)(2,1)}), (bf16[512,2048]{0,1:T(8,128)(2,1)}, bf16[512,2048]{0,1:T(8,128)(2,1)})) %all-reduce.3.cloned.1.call-update) | async-done | bytes 4194320 | tf_op jit(solution)/shard_map/psum | solution.py:20
  162.6 0.0 copy-done.1
  162.6 17.1 %fusion = f32[2048,4096]{1,0:T(8,128)} fusion(bf16[512,2048]{0,1:T(8,128)(2,1)S(1)} %copy-done.1, bf16[512,2048]{0,1:T(8,128)(2,1)} %get-tuple-element.8, bf16[512,2048]{0,1:T(8,128)(2,1)} %get-tuple-element.9), kind=kOutput, calls=%fused_computation | convolution fusion | flops 8598323200 | bytes 39845888 | tf_op jit(solution)/shard_map/dot_general | solution.py:75
  (4 shorter events, 0.0 us)
Async XLA Ops:
  7.2 3.2 %copy-start = (bf16[128,1024]{1,0:T(8,128)(2,1)S(1)}, bf16[128,1024]{1,0:T(8,128)(2,1)}, u32[]{:S(2)}) copy-start(bf16[128,1024]{1,0:T(8,128)(2,1)} %param.6) | copy-start | bytes 786436
  7.2 12.5 %copy-start.3 = (s32[128]{0:T(128)S(1)}, s32[128]{0:T(128)}, u32[]{:S(2)}) copy-start(s32[128]{0:T(128)} %param.7) | copy-start | bytes 1540
  7.2 72.3 %all-gather.2.cloned.1.call-start = ((), (), s32[]{:S(2)}) async-start(), calls=%async_computation | async-start | bytes 2621440 | tf_op jit(solution)/shard_map/all_gather | solution.py:69
  7.2 4.8 %collective-permute-start = (s32[128]{0:T(128)}, s32[128]{0:T(128)S(1)}, u32[]{:S(2)}, u32[]{:S(2)}) collective-permute-start(s32[128]{0:T(128)} %param.7), channel_id=1, source_target_pairs={{0,1},{1,0},{2,3},{3,2},{4,5},{5,4},{6,7},{7,6},{8,9},{9,8},{10,11... | collective-permute-start | bytes 1544 | tf_op jit(solution)/shard_map/ppermute | solution.py:15
  10.5 10.0 %collective-permute-start.4 = (bf16[128,128]{0,1:T(8,128)(2,1)S(1)}, bf16[128,128]{0,1:T(8,128)(2,1)S(1)}, u32[]{:S(2)}, u32[]{:S(2)}) collective-permute-start(bf16[128,128]{0,1:T(8,128)(2,1)S(1)} %copy.18), channel_id=1, source_target_pairs={{0,1},{1,0},{2,3},{3,2},{4,5},{5,4},{6,7},{7,6},{8,9},{9,8},{10,11... | collective-permute-start | bytes 98312 | tf_op jit(solution)/shard_map/ppermute | solution.py:15
  12.7 7.0 %collective-permute-start.1 = (s32[256]{0:T(256)S(1)}, s32[256]{0:T(256)S(1)}, u32[]{:S(2)}, u32[]{:S(2)}) collective-permute-start(s32[256]{0:T(256)S(1)} %pad_add_fusion.1), channel_id=1, source_target_pairs={{0,2},{1,3},{2,0},{3,1},{4,6},{5,7},{6,4},{7,5},{8,10},{9,11},{10,... | collective-permute-start | bytes 3080 | tf_op jit(solution)/shard_map/ppermute | solution.py:15
  16.5 3.9 %collective-permute-start.2 = (bf16[128,128]{1,0:T(8,128)(2,1)S(1)}, bf16[128,128]{1,0:T(8,128)(2,1)S(1)}, u32[]{:S(2)}, u32[]{:S(2)}) collective-permute-start(bf16[128,128]{1,0:T(8,128)(2,1)S(1)} %constant_dynamic-slice_fusion.1), channel_id=1, source_target_pairs={{0,1},{1,0},{2,3},{3,2},{4,5},{5,4},{6,7},{7,6},{8,9},{9,8},{10,11... | collective-permute-start | bytes 98312 | tf_op jit(solution)/shard_map/ppermute | solution.py:15
  20.4 5.2 %collective-permute-start.3 = (bf16[256,128]{1,0:T(8,128)(2,1)S(1)}, bf16[256,128]{1,0:T(8,128)(2,1)S(1)}, u32[]{:S(2)}, u32[]{:S(2)}) collective-permute-start(bf16[256,128]{1,0:T(8,128)(2,1)S(1)} %pad_maximum_fusion), channel_id=1, source_target_pairs={{0,2},{1,3},{2,0},{3,1},{4,6},{5,7},{6,4},{7,5},{8,10},{9,11},{10,... | collective-permute-start | bytes 196616 | tf_op jit(solution)/shard_map/ppermute | solution.py:15
  20.5 9.5 %collective-permute-start.5 = (bf16[256,128]{0,1:T(8,128)(2,1)S(1)}, bf16[256,128]{0,1:T(8,128)(2,1)S(1)}, u32[]{:S(2)}, u32[]{:S(2)}) collective-permute-start(bf16[256,128]{0,1:T(8,128)(2,1)S(1)} %pad_maximum_fusion.1), channel_id=1, source_target_pairs={{0,2},{1,3},{2,0},{3,1},{4,6},{5,7},{6,4},{7,5},{8,10},{9,11},{10,... | collective-permute-start | bytes 196616 | tf_op jit(solution)/shard_map/ppermute | solution.py:15
  33.2 129.4 %all-reduce.3.cloned.1.call-start = ((), (), s32[]{:S(2)}) async-start(), calls=%async_computation.1 | async-start | bytes 8388608 | tf_op jit(solution)/shard_map/psum | solution.py:20
  83.4 1.0 copy-start.2
  83.4 79.2 %copy-start.1 = (bf16[512,2048]{0,1:T(8,128)(2,1)S(1)}, bf16[512,2048]{0,1:T(8,128)(2,1)}, u32[]{:S(2)}) copy-start(bf16[512,2048]{0,1:T(8,128)(2,1)} %all-gather.2.cloned.1.call-done) | copy-start | bytes 6291460
Sparse Core Ops, SparseCore 0:
  33.3 46.0 all-gather.1
  83.5 79.0 all-reduce.2
where the time goes:
time: 187 us; the launch traced here: 186 us
  waiting for transfers between devices  127 us (68%)
  matrix products  21.2 us (11%)
  between operations  14.1 us (8%)
  starting transfers between devices  11.7 us (6%)
  local copies, waits for them, and re-layouts  7.29 us (4%)
  other arithmetic  5.39 us (3%)
    psum x1, waiting for transfers between devices, spread(): return lax.psum(jnp.where(mine, x, jnp.zeros_like(x)), axis)  77.2 us
    all_gather x1, waiting for transfers between devices, on_device(): row_operand = lax.all_gather(attended, 'seq', axis=0, tiled=True)  46.2 us
    dot_general x1, matrix products, on_device(): lax.dot_general(row_operand, columns, (((0,), (0,)), ((), ())), preferred...  17.1 us
    ppermute x6, starting transfers between devices, from_partner(): return lax.ppermute(value, axis, pairs)  11.6 us
    select_n x1, other arithmetic, spread(): return lax.psum(jnp.where(mine, x, jnp.zeros_like(x)), axis)  3.89 us
  transfers between devices with their start and end apart: 8, of which 5 were waited for; matrix products, arithmetic and copies ran while one was open for 5% of the time, Pallas kernels for 0%

commit v1 on v0

--- a/solution.py
+++ b/solution.py
@@ -9,6 +9,12 @@
 SPANS = 4
 
 
+def gather_and_add(shard, axis):
+    parts = lax.all_gather(shard, axis, axis=0, tiled=False)
+    total = parts.sum(axis=0)
+    return total
+
+
 def from_partner(value, axis, stride):
     mask = 2**stride
     pairs = [(source, source ^ mask) for source in range(lax.axis_size(axis))]
@@ -17,7 +23,7 @@
 
 def spread(x, axis, root):
     mine = lax.axis_index(axis) == root
-    return lax.psum(jnp.where(mine, x, jnp.zeros_like(x)), axis)
+    return gather_and_add(jnp.where(mine, x, jnp.zeros_like(x)), axis)
 
 
 def attend_block(queries, key_block, value_block, visible, local_heads, local_tokens, score_scale):

time: 187 us -> 331 us (1.77)
  waiting for transfers between devices: 127 us -> 217 us
  local copies, waits for them, and re-layouts: 7.29 us -> 41.9 us
  other arithmetic: 5.39 us -> 26.8 us
    all_gather x0 -> x2, waiting for transfers between devices: none -> 167 us  [gather_and_add(): parts = lax.all_gather(shard, axis, axis=0, tiled=False)]
    psum x1 -> x0, waiting for transfers between devices: 77.2 us -> none  [spread(): return lax.psum(jnp.where(mine, x, jnp.zeros_like(x)), axis)]
    unnamed x11 -> x15, local copies, waits for them, and re-layouts: 3.46 us -> 38.1 us
    reduce_sum x0 -> x1, other arithmetic: none -> 20 us  [gather_and_add(): total = parts.sum(axis=0)]
  transfers between devices with their start and end apart: 8 -> 9, of which waited for: 5 -> 5; matrix products, arithmetic and copies ran while one was open for 5% -> 8% of each run, Pallas kernels for 0% -> 0%
where the time goes in v1:
time: 331 us; the launch traced here: 330 us
  waiting for transfers between devices  217 us (66%)
  local copies, waits for them, and re-layouts  41.9 us (13%)
  other arithmetic  26.8 us (8%)
  matrix products  19 us (6%)
  between operations  13.9 us (4%)
  starting transfers between devices  12 us (4%)
    all_gather x2, waiting for transfers between devices, gather_and_add(): parts = lax.all_gather(shard, axis, axis=0, tiled=False)  167 us
    all_gather x1, waiting for transfers between devices, on_device(): row_operand = lax.all_gather(attended, 'seq', axis=0, tiled=True)  45.5 us
    unnamed x15, local copies, waits for them, and re-layouts  38.1 us
    reduce_sum x1, other arithmetic, gather_and_add(): total = parts.sum(axis=0)  20 us
    dot_general x1, matrix products, on_device(): lax.dot_general(row_operand, columns, (((0,), (0,)), ((), ())), preferred...  14.9 us
    ppermute x6, starting transfers between devices, from_partner(): return lax.ppermute(value, axis, pairs)  11.7 us
  transfers between devices with their start and end apart: 9, of which 5 were waited for; matrix products, arithmetic and copies ran while one was open for 8% of the time, Pallas kernels for 0%

profile of v1, /device:TPU:0, one launch (start us, length us, event | category | flops | bytes accessed | tf_op | source)
XLA Modules:
  0.0 330.4 jit_solution(494997660993604652)
XLA Ops:
  7.2 0.0 copy-start
  7.2 0.0 all-gather.6.cloned.1.call-start
  7.2 3.1 collective-permute-start
  10.3 0.0 copy-done
  10.4 0.1 copy.23
  10.5 0.9 collective-permute-start.4
  11.4 0.7 collective-permute-done
  12.0 0.7 pad_add_fusion.1
  12.7 3.0 collective-permute-start.1
  15.7 0.8 constant_dynamic-slice_fusion.1
  16.5 1.6 collective-permute-start.2
  18.1 1.3 copy.17
  19.4 0.3 copy.18
  19.7 0.0 collective-permute-done.1
  19.7 0.7 pad_add_fusion
  20.3 0.8 broadcast_compare_fusion
  21.1 0.0 collective-permute-done.2
  21.2 0.6 collective-permute-start.3
  21.8 0.0 collective-permute-done.4
  21.8 2.5 collective-permute-start.5
  24.2 2.9 collective-permute-done.3
  27.1 0.3 broadcast_in_dim.19
  27.4 1.0 fusion.20
  28.3 0.7 fusion.4
  29.0 2.5 copy.22
  31.5 0.0 collective-permute-done.5
  31.5 3.2 fusion.7
  34.7 0.0 all-gather.6.cloned.1.call-update
  34.7 0.0 all-gather.8.cloned.1.call-start
  34.8 0.0 copy-start.4
  34.8 45.5 %all-gather.6.cloned.1.call-done = bf16[512,2048]{0,1:T(8,128)(2,1)} async-done(((bf16[128,2048]{0,1:T(8,128)(2,1)}), bf16[512,2048]{0,1:T(8,128)(2,1)}) %all-gather.6.cloned.1.call-update) | async-done | bytes 2097168 | tf_op jit(solution)/shard_map/all_gather | solution.py:75
  80.3 3.9 %broadcast_select_fusion.1 = (bf16[512,2048]{0,1:T(8,128)(2,1)}, bf16[512,2048]{0,1:T(8,128)(2,1)}) fusion(bf16[512,2048]{0,1:T(8,128)(2,1)} %all-gather.6.cloned.1.call-done, pred[]{:T(512)S(6)} %eq.6, pred[]{:T(512)S(6)} %eq.7), kind=kLoop, calls=%fused_computation.11 | loop fusion | flops 2097152 | bytes 6291458 | tf_op jit(solution)/shard_map/jit(_where)/select_n | solution.py:26
  84.2 0.0 all-gather.8.cloned.1.call-update
  84.3 0.2 all-gather.10.cloned.1.call-start
  84.5 0.5 all-gather.10.cloned.1.call-update
  85.0 0.0 copy-done.4
  85.0 1.0 copy.21
  86.0 89.6 %all-gather.8.cloned.1.call-done = bf16[4096,2048]{0,1:T(8,128)(2,1)} async-done(((bf16[512,2048]{0,1:T(8,128)(2,1)}), bf16[4096,2048]{0,1:T(8,128)(2,1)}) %all-gather.8.cloned.1.call-update) | async-done | bytes 16777232 | tf_op jit(solution)/shard_map/all_gather | solution.py:13
  175.6 17.2 %copy.25 = bf16[256,8,8,512]{3,2,1,0:T(8,128)(2,1)} copy(bf16[256,8,8,512]{3,1,2,0:T(8,128)(2,1)} %bitcast.38) | data formatting | bytes 33554432
  192.8 77.7 %all-gather.10.cloned.1.call-done = bf16[4096,2048]{0,1:T(8,128)(2,1)} async-done(((bf16[512,2048]{0,1:T(8,128)(2,1)}), bf16[4096,2048]{0,1:T(8,128)(2,1)}) %all-gather.10.cloned.1.call-update) | async-done | bytes 16777232 | tf_op jit(solution)/shard_map/all_gather | solution.py:13
  270.6 0.0 copy-start.2
  270.6 18.4 %copy.26 = bf16[256,8,8,512]{3,2,1,0:T(8,128)(2,1)} copy(bf16[256,8,8,512]{3,1,2,0:T(8,128)(2,1)} %bitcast.39) | data formatting | bytes 33554432
  289.0 0.0 copy-done.2
  289.0 20.0 %bitcast_reduce_fusion = (bf16[512,2048]{0,1:T(8,128)(2,1)S(1)}, bf16[512,2048]{0,1:T(8,128)(2,1)S(1)}) fusion(bf16[256,8,8,512]{3,2,1,0:T(8,128)(2,1)} %copy.26, bf16[256,8,8,512]{3,2,1,0:T(8,128)(2,1)S(1)} %copy-done.2), kind=kLoop, calls=%fused_computation | loop fusion | flops 14680064 | bytes 37748736 | tf_op jit(solution)/shard_map/reduce_sum | solution.py:14
  309.0 0.0 copy-done.3
  309.0 0.0 copy-start.1
  309.0 14.9 %fusion = f32[2048,4096]{1,0:T(8,128)} fusion(bf16[512,2048]{0,1:T(8,128)(2,1)S(1)} %copy-done.3, bf16[512,2048]{0,1:T(8,128)(2,1)S(1)} %get-tuple-element.16, bf16[512,2048]{0,1:T(8,128)(2,1)S(1)} %get-tuple-element.17), kind=kOutput, calls=%fused_computation.2 | convolution fusion | flops 8598323200 | bytes 39845888 | tf_op jit(solution)/shard_map/dot_general | solution.py:81
  323.9 0.0 copy-done.1
  (4 shorter events, 0.0 us)
Async XLA Ops:
  7.2 3.2 copy-start
  7.2 73.1 %all-gather.6.cloned.1.call-start = ((), (), s32[]{:S(2)}) async-start(), calls=%async_computation | async-start | bytes 2621440 | tf_op jit(solution)/shard_map/all_gather | solution.py:75
  7.2 4.8 %collective-permute-start = (s32[128]{0:T(128)}, s32[128]{0:T(128)S(1)}, u32[]{:S(2)}, u32[]{:S(2)}) collective-permute-start(s32[128]{0:T(128)} %param.7), channel_id=1, source_target_pairs={{0,1},{1,0},{2,3},{3,2},{4,5},{5,4},{6,7},{7,6},{8,9},{9,8},{10,11... | collective-permute-start | bytes 1544 | tf_op jit(solution)/shard_map/ppermute | solution.py:21
  10.5 11.3 %collective-permute-start.4 = (bf16[128,128]{0,1:T(8,128)(2,1)S(1)}, bf16[128,128]{0,1:T(8,128)(2,1)S(1)}, u32[]{:S(2)}, u32[]{:S(2)}) collective-permute-start(bf16[128,128]{0,1:T(8,128)(2,1)S(1)} %copy.23), channel_id=1, source_target_pairs={{0,1},{1,0},{2,3},{3,2},{4,5},{5,4},{6,7},{7,6},{8,9},{9,8},{10,11... | collective-permute-start | bytes 98312 | tf_op jit(solution)/shard_map/ppermute | solution.py:21
  12.7 7.0 %collective-permute-start.1 = (s32[256]{0:T(256)S(1)}, s32[256]{0:T(256)S(1)}, u32[]{:S(2)}, u32[]{:S(2)}) collective-permute-start(s32[256]{0:T(256)S(1)} %pad_add_fusion.1), channel_id=1, source_target_pairs={{0,2},{1,3},{2,0},{3,1},{4,6},{5,7},{6,4},{7,5},{8,10},{9,11},{10,... | collective-permute-start | bytes 3080 | tf_op jit(solution)/shard_map/ppermute | solution.py:21
  16.5 4.7 %collective-permute-start.2 = (bf16[128,128]{1,0:T(8,128)(2,1)S(1)}, bf16[128,128]{1,0:T(8,128)(2,1)S(1)}, u32[]{:S(2)}, u32[]{:S(2)}) collective-permute-start(bf16[128,128]{1,0:T(8,128)(2,1)S(1)} %constant_dynamic-slice_fusion.1), channel_id=1, source_target_pairs={{0,1},{1,0},{2,3},{3,2},{4,5},{5,4},{6,7},{7,6},{8,9},{9,8},{10,11... | collective-permute-start | bytes 98312 | tf_op jit(solution)/shard_map/ppermute | solution.py:21
  21.2 5.9 %collective-permute-start.3 = (bf16[256,128]{1,0:T(8,128)(2,1)S(1)}, bf16[256,128]{1,0:T(8,128)(2,1)S(1)}, u32[]{:S(2)}, u32[]{:S(2)}) collective-permute-start(bf16[256,128]{1,0:T(8,128)(2,1)S(1)} %pad_maximum_fusion), channel_id=1, source_target_pairs={{0,2},{1,3},{2,0},{3,1},{4,6},{5,7},{6,4},{7,5},{8,10},{9,11},{10,... | collective-permute-start | bytes 196616 | tf_op jit(solution)/shard_map/ppermute | solution.py:21
  21.8 9.7 %collective-permute-start.5 = (bf16[256,128]{0,1:T(8,128)(2,1)S(1)}, bf16[256,128]{0,1:T(8,128)(2,1)S(1)}, u32[]{:S(2)}, u32[]{:S(2)}) collective-permute-start(bf16[256,128]{0,1:T(8,128)(2,1)S(1)} %pad_maximum_fusion.1), channel_id=1, source_target_pairs={{0,2},{1,3},{2,0},{3,1},{4,6},{5,7},{6,4},{7,5},{8,10},{9,11},{10,... | collective-permute-start | bytes 196616 | tf_op jit(solution)/shard_map/ppermute | solution.py:21
  34.7 140.9 %all-gather.8.cloned.1.call-start = ((), (), s32[]{:S(2)}) async-start(), calls=%async_computation.1 | async-start | bytes 18874368 | tf_op jit(solution)/shard_map/all_gather | solution.py:13
  34.8 50.2 %copy-start.4 = (bf16[128,16,128]{0,2,1:T(8,128)(2,1)S(1)}, bf16[128,16,128]{0,2,1:T(8,128)(2,1)}, u32[]{:S(2)}) copy-start(bf16[128,16,128]{0,2,1:T(8,128)(2,1)} %fusion.7) | copy-start | bytes 1572868
  84.3 186.3 %all-gather.10.cloned.1.call-start = ((), (), s32[]{:S(2)}) async-start(), calls=%async_computation.2 | async-start | bytes 18874368 | tf_op jit(solution)/shard_map/all_gather | solution.py:13
  270.6 18.4 %copy-start.2 = (bf16[256,8,8,512]{3,2,1,0:T(8,128)(2,1)S(1)}, bf16[256,8,8,512]{3,2,1,0:T(8,128)(2,1)}, u32[]{:S(2)}) copy-start(bf16[256,8,8,512]{3,2,1,0:T(8,128)(2,1)} %copy.25) | copy-start | bytes 50331652
  289.0 20.1 %copy-start.3 = (bf16[512,2048]{0,1:T(8,128)(2,1)S(1)}, bf16[512,2048]{0,1:T(8,128)(2,1)}, u32[]{:S(2)}) copy-start(bf16[512,2048]{0,1:T(8,128)(2,1)} %all-gather.6.cloned.1.call-done) | copy-start | bytes 6291460
  309.0 14.9 %copy-start.1 = (bf16[128,1024]{1,0:T(8,128)(2,1)S(1)}, bf16[128,1024]{1,0:T(8,128)(2,1)}, u32[]{:S(2)}) copy-start(bf16[128,1024]{1,0:T(8,128)(2,1)} %param.6) | copy-start | bytes 786436
Sparse Core Ops, SparseCore 0:
  34.9 45.3 all-gather.5
  84.4 91.1 all-gather.7
  177.5 93.0 all-gather.9
